TPU v7x, 128 devices: a whole 4x4x4 slice. The times are simulated.
128 devices in a mesh: expert: 8 (over z, core), fsdp: 16 (over y, x).
Axes of the slice: x: 4, y: 4, z: 4, core: 2. Of those that a mesh axis runs over, the one named last changes fastest.
Arguments:
- hidden: bfloat16 [8, 768, 8192], P('expert', None, 'fsdp'), may hold values from -0.198873782 to 0.198873782
- expert_ids: int32 [2048, 2], P(('expert', 'fsdp')), may hold values from 0 to 7, all different within a row; in each aligned block of 16 rows (0 to 15, 16 to 31, ...) at most 6 rows name the same one
- gate_weights: float32 [2048, 2], P(('expert', 'fsdp')), may hold values from 0.2 to 1
- loss_weight: float32 [2048], P(('expert', 'fsdp')), may hold values from 0.3 to 3
- decay: float32 [1], replicated, may hold values from 0.2 to 0.6
- val_grad: bfloat16 [8, 8192, 4096], P('expert', 'fsdp'), may hold values from -8 to 8
- down_weight: bfloat16 [8, 8192, 4096], P('expert', 'fsdp'), may hold values from -0.0625 to 0.0625
Outputs:
- solution: float32 [8, 8192, 4096], P('expert', 'fsdp')
- hyper: float32 [1], replicated
Inputs may be any that keep to these rules, and one draw needn't show every extreme that they name: `expert_ids`: each token names 2 different experts; among the 16 tokens of one device no expert is named more than 6 times, a bound that some block reaches.
All inputs are finite; a program needn't handle non-finite values.
Results may differ from a plain program's by a relative error of at most 0.00067.
Values may be sent and summed in bfloat16 or wider, within the bound.
No kernel may reach another device: no remote copies, remote signals or barrier semaphores. Data moves between devices by JAX's collectives and lax.ppermute only.
A program may use at most 128 MiB of HBM per device.

v0:
```python
import math
import jax
import jax.numpy as jnp
from jax import lax
from jax.sharding import Mesh
from jax.sharding import PartitionSpec as P

D = 4096
ITERS = 2
EXPERT_FSDP = ("expert_0", "expert_1", "fsdp_0", "fsdp_1")
EXPERT = ("expert_0", "expert_1")
FSDP = ("fsdp_0", "fsdp_1")


def by_axis(array, axes):
    for axis in axes:
        array = lax.psum(array, axis)
    return array


def gate_table(expert_ids, gate_weights, experts, capacity):
    flat_ids = expert_ids.reshape(-1)
    labels = jnp.arange(experts, dtype=jnp.int32)
    onehot = (flat_ids[:, None] == labels[None, :]).astype(jnp.int32)
    earlier = jnp.cumsum(onehot, axis=0) - onehot
    slots = jnp.sum(earlier * onehot, axis=1)
    targets = flat_ids * capacity + slots
    columns = jnp.arange(experts * capacity, dtype=jnp.int32)
    hits = (targets[:, None] == columns[None, :]).astype(jnp.float32)
    weighted = hits * gate_weights.reshape(-1)[:, None]
    return jnp.sum(weighted.reshape(-1, expert_ids.shape[1], experts * capacity), axis=1)


def combine(table, weights, outputs):
    mixed = jnp.dot(
        table, outputs, precision=lax.Precision.HIGHEST, preferred_element_type=jnp.float32
    )
    scaled = weights[:, None] * mixed
    back = jnp.dot(
        table.T, scaled, precision=lax.Precision.HIGHEST, preferred_element_type=jnp.float32
    )
    return back.astype(jnp.bfloat16)


def joined_sums(residual, direction, image, target):
    return (
        by_axis(jnp.sum(residual * residual), EXPERT_FSDP),
        by_axis(jnp.sum(direction * image), EXPERT_FSDP),
        by_axis(jnp.sum(residual * image), EXPERT_FSDP),
        by_axis(jnp.sum(image * image), EXPERT_FSDP),
        by_axis(jnp.sum(target.astype(jnp.float32) * direction), EXPERT_FSDP),
    )


def local(hidden, expert_ids, gate_weights, loss_weight, decay, val_grad, down_weight):
    n_expert = lax.axis_size(EXPERT)
    n_fsdp = lax.axis_size(FSDP)
    capacity = hidden.shape[1] // (n_expert * n_fsdp)
    decay_rate = decay[0]
    table = gate_table(expert_ids, gate_weights, n_expert, capacity)
    local_hidden = hidden[0]
    right_side, target = (val_grad, down_weight)
    start_side = right_side.astype(jnp.float32)
    solution = jnp.zeros_like(start_side)
    residual = start_side
    direction = start_side
    along_total = jnp.float32(0.0)
    for iteration in range(ITERS):
        if iteration > 0:
            direction = residual + norm_guess / norm_prev * direction
        rounded = direction[0].astype(jnp.bfloat16)
        summed = lax.psum_scatter(
            jnp.dot(local_hidden, rounded, preferred_element_type=jnp.float32),
            FSDP,
            scatter_dimension=0,
            tiled=True,
        )
        arrived = lax.all_to_all(summed, EXPERT, split_axis=0, concat_axis=0, tiled=True)
        leaving = combine(table, loss_weight, arrived)
        returned = lax.all_to_all(leaving, EXPERT, split_axis=0, concat_axis=0, tiled=True)
        gradient = lax.dot_general(
            local_hidden,
            lax.all_gather(returned, FSDP, axis=0, tiled=True),
            (((0,), (0,)), ((), ())),
            preferred_element_type=jnp.float32,
        )
        image = gradient[None] + decay_rate * direction
        norm_now, curve, cross, square, along = joined_sums(residual, direction, image, target)
        alpha = norm_now / curve
        solution = solution + alpha * direction
        residual = residual - alpha * image
        norm_guess = norm_now - 2.0 * alpha * cross + alpha * alpha * square
        norm_prev = norm_now
        along_total = along_total + alpha * along
    hyper = -along_total / math.sqrt(n_expert * D)
    return (solution, jnp.reshape(hyper, (1,)))


def solution(mesh):
    finer = Mesh(mesh.devices.reshape(4, 2, 4, 4), ("expert_0", "expert_1", "fsdp_0", "fsdp_1"))
    placed = (
        P(EXPERT, None, FSDP),
        P(EXPERT_FSDP, None),
        P(EXPERT_FSDP, None),
        P(EXPERT_FSDP),
        P(),
        P(EXPERT, FSDP, None),
        P(EXPERT, FSDP, None),
    )
    return jax.shard_map(
        local, mesh=finer, in_specs=placed, out_specs=(P(EXPERT, FSDP, None), P()), check_vma=False
    )
```

profile of v0, /device:TPU:0, one launch (start us, length us, event | category | flops | bytes accessed | tf_op | source)
XLA Modules:
  0.0 544.2 jit_solution(16271983358100491739)
XLA Ops:
  8.3 8.6 %fusion.10 = f32[768,4096]{1,0:T(8,128)} fusion(bf16[1,512,4096]{2,1,0:T(8,128)(2,1)} %param.12, bf16[1,768,512]{2,1,0:T(8,128)(2,1)S(1)} %copy-done), kind=kOutput, calls=%fused_computation.26 | convolution fusion | flops 3221225472 | bytes 17563648 | tf_op jit(solution)/shard_map/dot_general | solution.py:73
  16.9 97.7 %reduce-scatter.5.cloned.1.call-done = f32[48,4096]{1,0:T(8,128)} async-done(((f32[768,4096]{1,0:T(8,128)}), f32[48,4096]{1,0:T(8,128)}) %reduce-scatter.5.cloned.1.call-update) | async-done | bytes 786448 | tf_op jit(solution)/shard_map/reduce_scatter | solution.py:72
  122.0 15.1 %all-to-all-done = f32[8,6,4096]{2,1,0:T(8,128)S(1)} async-done(((f32[8,6,4096]{2,1,0:T(8,128)}), f32[8,6,4096]{2,1,0:T(8,128)S(1)}, u32[]{:S(2)}, u32[]{:S(2)}) %all-to-all-start) | async-done | bytes 786464 | tf_op jit(solution)/shard_map/all_to_all | solution.py:78
  138.7 12.8 %all_to_all.48 = bf16[8,6,4096]{2,1,0:T(8,128)(2,1)S(1)} all-to-all(bf16[8,6,4096]{2,1,0:T(8,128)(2,1)S(1)} %all_to_all.35), channel_id=1, replica_groups=mesh['expert_0'=4,'expert_1'=2,'fsdp_0'=4,'fsdp_1'=4] {'expert_0','exper..., dimensions={0} | all-to-all | bytes 786432 | tf_op jit(solution)/shard_map/all_to_all | solution.py:80
  152.4 6.5 %copy.40 = bf16[1,512,4096]{1,2,0:T(8,128)(2,1)} copy(bf16[1,512,4096]{2,1,0:T(8,128)(2,1)} %param.12) | data formatting | bytes 8388608 | tf_op args[5]
  159.6 51.1 %all-gather.3.cloned.1.call-done = bf16[768,4096]{1,0:T(8,128)(2,1)} async-done(((bf16[48,4096]{1,0:T(8,128)(2,1)}), bf16[768,4096]{1,0:T(8,128)(2,1)}) %all-gather.3.cloned.1.call-update) | async-done | bytes 6291472 | tf_op jit(solution)/shard_map/all_gather | solution.py:83
  210.7 12.3 %multiply_reduce_fusion = (f32[]{:T(128)}, f32[]{:T(128)}, f32[]{:T(128)}, f32[1,512,4096]{1,2,0:T(8,128)}) fusion(bf16[1,512,4096]{1,2,0:T(8,128)(2,1)} %copy.40, f32[]{:T(128)} %bitcast.44, bf16[768,4096]{1,0:T(8,128)(2,1)} %all-gather.3.cloned.1.call-done, bf16[1,768,512]{2,1,0:T(8,128)(2,1)S(1)} %copy-done), kind=kOutput, calls=%fused_computation.18 | convolution fusion | flops 3240099840 | bytes 19660816 | tf_op jit(solution)/shard_map/dot_general | solution.py:81
  222.9 11.4 %all-reduce.5 = (f32[]{:T(128)}, f32[]{:T(128)}, f32[]{:T(128)}) all-reduce(f32[]{:T(128)} %get-tuple-element.17, f32[]{:T(128)} %get-tuple-element.16, f32[]{:T(128)} %get-tuple-element.15), channel_id=1, replica_groups=mesh['expert_0'=4,'expert_1'=2,'fsdp_0'=4,'fsdp_1'=4] {'expert_0'}, use_global_device_ids=true, to_apply=%region_1.2 | all-reduce | flops 3 | bytes 24 | tf_op jit(solution)/shard_map/psum | solution.py:17
  237.4 11.1 %all-reduce.3 = (f32[]{:T(128)}, f32[]{:T(128)}, f32[]{:T(128)}) all-reduce(f32[]{:T(128)} %get-tuple-element.43, f32[]{:T(128)} %get-tuple-element.44, f32[]{:T(128)} %get-tuple-element.45), channel_id=1, replica_groups=mesh['expert_0'=4,'expert_1'=2,'fsdp_0'=4,'fsdp_1'=4] {'fsdp_0'}, use_global_device_ids=true, to_apply=%region_3.4 | all-reduce | flops 3 | bytes 24 | tf_op jit(solution)/shard_map/psum | solution.py:17
  248.5 9.4 %all-reduce.1 = (f32[]{:T(128)}, f32[]{:T(128)}, f32[]{:T(128)}) all-reduce(f32[]{:T(128)} %get-tuple-element.29, f32[]{:T(128)} %get-tuple-element.30, f32[]{:T(128)} %get-tuple-element.31), channel_id=1, replica_groups=mesh['expert_0'=4,'expert_1'=2,'fsdp_0'=4,'fsdp_1'=4] {'fsdp_1'}, use_global_device_ids=true, to_apply=%region_4.5 | all-reduce | flops 3 | bytes 24 | tf_op jit(solution)/shard_map/psum | solution.py:17
  261.8 13.1 %convolution_bitcast_fusion = f32[768,4096]{0,1:T(8,128)} fusion(bf16[1,768,512]{2,1,0:T(8,128)(2,1)S(1)} %copy-done, bf16[1,512,4096]{1,2,0:T(8,128)(2,1)} %copy.40, f32[1,512,4096]{1,2,0:T(8,128)} %get-tuple-element.46, f32[]{:T(128)S(6)} %div.13, f32[]{:T(128)S(6)} %div.12), kind=kOutput, calls=%fused_computation.20 | convolution fusion | flops 3233808384 | bytes 25952264 | tf_op jit(solution)/shard_map/dot_general | solution.py:73
  274.9 12.6 %copy.46 = f32[768,4096]{1,0:T(8,128)} copy(f32[768,4096]{0,1:T(8,128)} %convolution_bitcast_fusion) | data formatting | bytes 25165824
  287.6 89.8 %reduce-scatter.7.cloned.1.call-done = f32[48,4096]{1,0:T(8,128)} async-done(((f32[768,4096]{1,0:T(8,128)}), f32[48,4096]{1,0:T(8,128)}) %reduce-scatter.7.cloned.1.call-update) | async-done | bytes 786448 | tf_op jit(solution)/shard_map/reduce_scatter | solution.py:72
  378.6 20.2 %all_to_all.49 = f32[8,6,4096]{2,1,0:T(8,128)S(1)} all-to-all(f32[8,6,4096]{2,1,0:T(8,128)S(1)} %all_to_all.38), channel_id=1, replica_groups=mesh['expert_0'=4,'expert_1'=2,'fsdp_0'=4,'fsdp_1'=4] {'expert_0','exper..., dimensions={0} | all-to-all | bytes 1572864 | tf_op jit(solution)/shard_map/all_to_all | solution.py:78
  400.4 12.8 %all_to_all.50 = bf16[8,6,4096]{2,1,0:T(8,128)(2,1)S(1)} all-to-all(bf16[8,6,4096]{2,1,0:T(8,128)(2,1)S(1)} %all_to_all.41), channel_id=1, replica_groups=mesh['expert_0'=4,'expert_1'=2,'fsdp_0'=4,'fsdp_1'=4] {'expert_0','exper..., dimensions={0} | all-to-all | bytes 786432 | tf_op jit(solution)/shard_map/all_to_all | solution.py:80
  414.1 6.6 %copy.44 = bf16[1,512,4096]{1,2,0:T(8,128)(2,1)} copy(bf16[1,512,4096]{2,1,0:T(8,128)(2,1)} %param.13) | data formatting | bytes 8388608 | tf_op args[6]
  420.7 8.4 %fusion = (f32[]{:T(128)}, f32[]{:T(128)}, f32[]{:T(128)}) fusion(bf16[1,512,4096]{1,2,0:T(8,128)(2,1)} %copy.44, f32[]{:T(128)S(6)} %div.13, f32[1,512,4096]{1,2,0:T(8,128)} %get-tuple-element.46, f32[]{:T(128)S(6)} %div.12, bf16[1,512,4096]{1,2,0:T(8,128)(2,1)} %copy.40), kind=kLoop, calls=%fused_computation.8 | loop fusion | flops 25165824 | bytes 16777236 | tf_op jit(solution)/shard_map/reduce_sum | solution.py:51
  429.0 43.4 %all-gather.5.cloned.1.call-done = bf16[768,4096]{1,0:T(8,128)(2,1)} async-done(((bf16[48,4096]{1,0:T(8,128)(2,1)}), bf16[768,4096]{1,0:T(8,128)(2,1)}) %all-gather.5.cloned.1.call-update) | async-done | bytes 6291472 | tf_op jit(solution)/shard_map/all_gather | solution.py:83
  472.4 10.1 %fusion.8 = f32[]{:T(128)} fusion(bf16[768,4096]{1,0:T(8,128)(2,1)} %all-gather.5.cloned.1.call-done, f32[]{:T(128)} %bitcast.45, bf16[1,768,512]{2,1,0:T(8,128)(2,1)S(1)} %copy-done, f32[]{:T(128)S(6)} %div.13, f32[1,512,4096]{1,2,0:T(8,128)} %get-tuple-element.46, f32[]{:T(128)S(6)} %div.12, bf16[1,512,4096]{1,2,0:T(8,128)(2,1)} %copy.40), kind=kOutput, calls=%fused_computation.17 | convolution fusion | flops 3240099840 | bytes 19660816 | tf_op jit(solution)/shard_map/dot_general | solution.py:81
  482.5 11.4 %all-reduce.4 = (f32[]{:T(128)}, f32[]{:T(128)}, f32[]{:T(128)}, f32[]{:T(128)}) all-reduce(f32[]{:T(128)} %get-tuple-element.13, f32[]{:T(128)} %fusion.8, f32[]{:T(128)} %get-tuple-element.14, f32[]{:T(128)} %get-tuple-element.12), channel_id=1, replica_groups=mesh['expert_0'=4,'expert_1'=2,'fsdp_0'=4,'fsdp_1'=4] {'expert_0'}, use_global_device_ids=true, to_apply=%region_15.16 | all-reduce | flops 4 | bytes 32 | tf_op jit(solution)/shard_map/psum | solution.py:17
  497.0 11.1 %all-reduce.2 = (f32[]{:T(128)}, f32[]{:T(128)}, f32[]{:T(128)}, f32[]{:T(128)}) all-reduce(f32[]{:T(128)} %get-tuple-element.39, f32[]{:T(128)} %get-tuple-element.40, f32[]{:T(128)} %get-tuple-element.41, f32[]{:T(128)} %get-tuple-element.42), channel_id=1, replica_groups=mesh['expert_0'=4,'expert_1'=2,'fsdp_0'=4,'fsdp_1'=4] {'fsdp_0'}, use_global_device_ids=true, to_apply=%region_17.18 | all-reduce | flops 4 | bytes 32 | tf_op jit(solution)/shard_map/psum | solution.py:17
  508.1 9.2 %all-reduce = (f32[]{:T(128)}, f32[]{:T(128)}, f32[]{:T(128)}, f32[]{:T(128)}) all-reduce(f32[]{:T(128)} %get-tuple-element.25, f32[]{:T(128)} %get-tuple-element.26, f32[]{:T(128)} %get-tuple-element.27, f32[]{:T(128)} %get-tuple-element.28), channel_id=1, replica_groups=mesh['expert_0'=4,'expert_1'=2,'fsdp_0'=4,'fsdp_1'=4] {'fsdp_1'}, use_global_device_ids=true, to_apply=%region_18.19 | all-reduce | flops 4 | bytes 32 | tf_op jit(solution)/shard_map/psum | solution.py:17
  518.7 7.7 %fusion.4 = f32[1,512,4096]{1,2,0:T(8,128)} fusion(bf16[1,512,4096]{1,2,0:T(8,128)(2,1)} %copy.40, f32[]{:T(128)S(6)} %div.14, f32[]{:T(128)S(6)} %div.12, f32[]{:T(128)S(6)} %div.13, f32[1,512,4096]{1,2,0:T(8,128)} %get-tuple-element.46), kind=kLoop, calls=%fused_computation.12 | loop fusion | flops 16777216 | bytes 20971532 | tf_op jit(solution)/shard_map/add | solution.py:90
  527.6 8.9 %copy.45 = f32[1,512,4096]{2,1,0:T(8,128)} copy(f32[1,512,4096]{1,2,0:T(8,128)} %fusion.4) | data formatting | bytes 16777216
  (40 shorter events, 21.1 us)
Async XLA Ops:
  7.2 1.1 copy-start
  7.2 107.4 %reduce-scatter.5.cloned.1.call-start = ((), (), s32[]{:S(2)}) async-start(), calls=%async_computation.6 | async-start | bytes 13369344 | tf_op jit(solution)/shard_map/reduce_scatter | solution.py:72
  16.9 104.4 %copy-start.1 = (s32[16,2]{0,1:T(2,128)S(1)}, s32[16,2]{0,1:T(2,128)}, u32[]{:S(2)}) copy-start(s32[16,2]{0,1:T(2,128)} %param.8) | copy-start | bytes 388
  16.9 105.0 %copy-start.3 = (f32[16,2]{0,1:T(2,128)S(1)}, f32[16,2]{0,1:T(2,128)}, u32[]{:S(2)}) copy-start(f32[16,2]{0,1:T(2,128)} %param.9) | copy-start | bytes 388
  16.9 120.4 %copy-start.2 = (f32[16]{0:T(128)S(1)}, f32[16]{0:T(128)}, u32[]{:S(2)}) copy-start(f32[16]{0:T(128)} %param.10) | copy-start | bytes 196
  116.7 20.4 %all-to-all-start = ((f32[8,6,4096]{2,1,0:T(8,128)}), f32[8,6,4096]{2,1,0:T(8,128)S(1)}, u32[]{:S(2)}, u32[]{:S(2)}) async-start(f32[8,6,4096]{2,1,0:T(8,128)} %all_to_all.32), calls=%async_computation.1 | async-start | bytes 2097152 | tf_op jit(solution)/shard_map/all_to_all | solution.py:78
  121.2 89.5 %all-gather.3.cloned.1.call-start = ((), (), s32[]{:S(2)}) async-start(), calls=%async_computation.7 | async-start | bytes 6684672 | tf_op jit(solution)/shard_map/all_gather | solution.py:83
  152.4 225.0 %reduce-scatter.7.cloned.1.call-start = ((), (), s32[]{:S(2)}) async-start(), calls=%async_computation.9 | async-start | bytes 13369344 | tf_op jit(solution)/shard_map/reduce_scatter | solution.py:72
  287.5 184.9 %all-gather.5.cloned.1.call-start = ((), (), s32[]{:S(2)}) async-start(), calls=%async_computation.8 | async-start | bytes 6684672 | tf_op jit(solution)/shard_map/all_gather | solution.py:83
Sparse Core Ops, SparseCore 0:
  17.0 97.4 reduce-scatter.4
  152.5 58.1 all-gather.2
  287.6 89.6 reduce-scatter.6
  414.2 58.1 all-gather.4
where the time goes:
time: 545 us; the launch traced here: 544 us
  waiting for transfers between devices  297 us (54%)
  blocking collectives  116 us (21%)
  matrix products  46.6 us (9%)
  local copies, waits for them, and re-layouts  41.8 us (8%)
  between operations  22 us (4%)
  other arithmetic  16.5 us (3%)
    reduce_scatter x2, waiting for transfers between devices, local(): lax.psum_scatter(jnp.dot(local_hidden, rounded, preferred_element_type=jn...  187 us
    all_gather x2, waiting for transfers between devices, local(): lax.all_gather(returned, FSDP, axis=0, tiled=True)  94.5 us
    psum x8, blocking collectives, by_axis(): array = lax.psum(array, axis)  69.9 us
    unnamed x13, local copies, waits for them, and re-layouts  35.8 us
    all_to_all x2, blocking collectives, local(): lax.all_to_all(leaving, EXPERT, split_axis=0, concat_axis=0, tiled=True)  25.5 us
    dot_general x2, matrix products, local(): lax.dot_general(local_hidden, lax.all_gather(returned, FSDP, axis=0, tile...  22.3 us
    dot_general x2, matrix products, local(): jnp.dot(local_hidden, rounded, preferred_element_type=jnp.float32)  21.6 us
    all_to_all x1, blocking collectives, local(): lax.all_to_all(summed, EXPERT, split_axis=0, concat_axis=0, tiled=True)  20.2 us
  transfers between devices with their start and end apart: 5, of which 5 were waited for; matrix products, arithmetic and copies ran while one was open for 4% of the time, Pallas kernels for 0%

commit v1 on v0

--- a/solution.py
+++ b/solution.py
@@ -14,7 +14,8 @@
 
 def by_axis(array, axes):
     for axis in axes:
-        array = lax.psum(array, axis)
+        pieces = lax.all_gather(array, axis, axis=0, tiled=False)
+        array = pieces.sum(axis=0)
     return array
 
 

time: 545 us -> 595 us (1.092)
  local copies, waits for them, and re-layouts: 41.8 us -> 83.5 us
  other arithmetic: 16.5 us -> 33.9 us
  blocking collectives: 116 us -> 110 us
    psum x8 -> x0, blocking collectives: 69.9 us -> none  [by_axis(): array = lax.psum(array, axis)]
    unnamed x0 -> x8, blocking collectives: none -> 64.3 us
    unnamed x13 -> x81, local copies, waits for them, and re-layouts: 35.8 us -> 77.5 us
    reduce_sum x0 -> x28, other arithmetic: none -> 17.4 us  [by_axis(): array = pieces.sum(axis=0)]
  transfers between devices with their start and end apart: 5 -> 5, of which waited for: 5 -> 5; matrix products, arithmetic and copies ran while one was open for 4% -> 5% of each run, Pallas kernels for 0% -> 0%
where the time goes in v1:
time: 595 us; the launch traced here: 593 us
  waiting for transfers between devices  292 us (49%)
  blocking collectives  110 us (18%)
  local copies, waits for them, and re-layouts  83.5 us (14%)
  matrix products  46.6 us (8%)
  other arithmetic  33.9 us (6%)
  between operations  22.2 us (4%)
    reduce_scatter x2, waiting for transfers between devices, local(): lax.psum_scatter(jnp.dot(local_hidden, rounded, preferred_element_type=jn...  188 us
    all_gather x2, waiting for transfers between devices, local(): lax.all_gather(returned, FSDP, axis=0, tiled=True)  89.5 us
    unnamed x81, local copies, waits for them, and re-layouts  77.5 us
    unnamed x8, blocking collectives  64.3 us
    all_to_all x2, blocking collectives, local(): lax.all_to_all(leaving, EXPERT, split_axis=0, concat_axis=0, tiled=True)  25.5 us
    dot_general x2, matrix products, local(): lax.dot_general(local_hidden, lax.all_gather(returned, FSDP, axis=0, tile...  22.4 us
    dot_general x2, matrix products, local(): jnp.dot(local_hidden, rounded, preferred_element_type=jnp.float32)  21.6 us
    all_to_all x1, blocking collectives, local(): lax.all_to_all(summed, EXPERT, split_axis=0, concat_axis=0, tiled=True)  20.2 us
  transfers between devices with their start and end apart: 5, of which 5 were waited for; matrix products, arithmetic and copies ran while one was open for 5% of the time, Pallas kernels for 0%

profile of v1, /device:TPU:0, one launch (start us, length us, event | category | flops | bytes accessed | tf_op | source)
XLA Modules:
  0.0 593.4 jit_solution(5223426219740897996)
XLA Ops:
  8.3 8.6 %fusion.10 = f32[768,4096]{1,0:T(8,128)} fusion(bf16[1,512,4096]{2,1,0:T(8,128)(2,1)} %param.12, bf16[1,768,512]{2,1,0:T(8,128)(2,1)S(1)} %copy-done), kind=kOutput, calls=%fused_computation.26 | convolution fusion | flops 3221225472 | bytes 17563648 | tf_op jit(solution)/shard_map/dot_general | solution.py:74
  16.9 97.7 %reduce-scatter.5.cloned.1.call-done = f32[48,4096]{1,0:T(8,128)} async-done(((f32[768,4096]{1,0:T(8,128)}), f32[48,4096]{1,0:T(8,128)}) %reduce-scatter.5.cloned.1.call-update) | async-done | bytes 786448 | tf_op jit(solution)/shard_map/reduce_scatter | solution.py:73
  122.1 15.1 %all-to-all-done = f32[8,6,4096]{2,1,0:T(8,128)S(1)} async-done(((f32[8,6,4096]{2,1,0:T(8,128)}), f32[8,6,4096]{2,1,0:T(8,128)S(1)}, u32[]{:S(2)}, u32[]{:S(2)}) %all-to-all-start) | async-done | bytes 786464 | tf_op jit(solution)/shard_map/all_to_all | solution.py:79
  138.8 12.8 %all_to_all.48 = bf16[8,6,4096]{2,1,0:T(8,128)(2,1)S(1)} all-to-all(bf16[8,6,4096]{2,1,0:T(8,128)(2,1)S(1)} %all_to_all.35), channel_id=1, replica_groups=mesh['expert_0'=4,'expert_1'=2,'fsdp_0'=4,'fsdp_1'=4] {'expert_0','exper..., dimensions={0} | all-to-all | bytes 786432 | tf_op jit(solution)/shard_map/all_to_all | solution.py:81
  152.6 6.5 %copy.40 = bf16[1,512,4096]{1,2,0:T(8,128)(2,1)} copy(bf16[1,512,4096]{2,1,0:T(8,128)(2,1)} %param.12) | data formatting | bytes 8388608 | tf_op args[5]
  160.4 50.5 %all-gather.3.cloned.1.call-done = bf16[768,4096]{1,0:T(8,128)(2,1)} async-done(((bf16[48,4096]{1,0:T(8,128)(2,1)}), bf16[768,4096]{1,0:T(8,128)(2,1)}) %all-gather.3.cloned.1.call-update) | async-done | bytes 6291472 | tf_op jit(solution)/shard_map/all_gather | solution.py:84
  210.8 12.3 %multiply_reduce_fusion = (f32[]{:T(128)}, f32[]{:T(128)}, f32[]{:T(128)}, f32[1,512,4096]{1,2,0:T(8,128)}) fusion(bf16[1,512,4096]{1,2,0:T(8,128)(2,1)} %copy.40, f32[]{:T(128)} %bitcast.76, bf16[768,4096]{1,0:T(8,128)(2,1)} %all-gather.3.cloned.1.call-done, bf16[1,768,512]{2,1,0:T(8,128)(2,1)S(1)} %copy-done), kind=kOutput, calls=%fused_computation.18 | convolution fusion | flops 3240099840 | bytes 19660816 | tf_op jit(solution)/shard_map/dot_general | solution.py:82
  227.9 10.7 %all-reduce.33 = (f32[4]{0:T(128)S(1)}, f32[4]{0:T(128)S(1)}, f32[4]{0:T(128)S(1)}) all-reduce(f32[4]{0:T(128)S(1)} %dynamic-update-slice, f32[4]{0:T(128)S(1)} %dynamic-update-slice.4, f32[4]{0:T(128)S(1)} %dynamic-update-slice.12), channel_id=1, replica_groups=mesh['expert_0'=4,'expert_1'=2,'fsdp_0'=4,'fsdp_1'=4] {'expert_0'}, use_global_device_ids=true, to_apply=%add | all-reduce | flops 12 | bytes 96
  254.7 10.4 %all-reduce.31 = (f32[4]{0:T(128)S(1)}, f32[4]{0:T(128)S(1)}, f32[4]{0:T(128)S(1)}) all-reduce(f32[4]{0:T(128)S(1)} %dynamic-update-slice.2, f32[4]{0:T(128)S(1)} %dynamic-update-slice.6, f32[4]{0:T(128)S(1)} %dynamic-update-slice.14), channel_id=1, replica_groups=mesh['expert_0'=4,'expert_1'=2,'fsdp_0'=4,'fsdp_1'=4] {'fsdp_0'}, use_global_device_ids=true, to_apply=%add.2 | all-reduce | flops 12 | bytes 96
  271.1 8.7 %all-reduce.29 = (f32[4]{0:T(128)S(1)}, f32[4]{0:T(128)S(1)}, f32[4]{0:T(128)S(1)}) all-reduce(f32[4]{0:T(128)S(1)} %dynamic-update-slice.3, f32[4]{0:T(128)S(1)} %dynamic-update-slice.7, f32[4]{0:T(128)S(1)} %dynamic-update-slice.15), channel_id=1, replica_groups=mesh['expert_0'=4,'expert_1'=2,'fsdp_0'=4,'fsdp_1'=4] {'fsdp_1'}, use_global_device_ids=true, to_apply=%add.3 | all-reduce | flops 12 | bytes 96
  285.6 13.1 %convolution_bitcast_fusion = f32[768,4096]{0,1:T(8,128)} fusion(bf16[1,768,512]{2,1,0:T(8,128)(2,1)S(1)} %copy-done, bf16[1,512,4096]{1,2,0:T(8,128)(2,1)} %copy.40, f32[1,512,4096]{1,2,0:T(8,128)} %get-tuple-element.46, f32[]{:T(128)S(6)} %div.13, f32[]{:T(128)S(6)} %div.12), kind=kOutput, calls=%fused_computation.20 | convolution fusion | flops 3233808384 | bytes 25952264 | tf_op jit(solution)/shard_map/dot_general | solution.py:74
  298.6 12.6 %copy.46 = f32[768,4096]{1,0:T(8,128)} copy(f32[768,4096]{0,1:T(8,128)} %convolution_bitcast_fusion) | data formatting | bytes 25165824
  311.3 90.0 %reduce-scatter.7.cloned.1.call-done = f32[48,4096]{1,0:T(8,128)} async-done(((f32[768,4096]{1,0:T(8,128)}), f32[48,4096]{1,0:T(8,128)}) %reduce-scatter.7.cloned.1.call-update) | async-done | bytes 786448 | tf_op jit(solution)/shard_map/reduce_scatter | solution.py:73
  402.6 20.2 %all_to_all.49 = f32[8,6,4096]{2,1,0:T(8,128)S(1)} all-to-all(f32[8,6,4096]{2,1,0:T(8,128)S(1)} %all_to_all.38), channel_id=1, replica_groups=mesh['expert_0'=4,'expert_1'=2,'fsdp_0'=4,'fsdp_1'=4] {'expert_0','exper..., dimensions={0} | all-to-all | bytes 1572864 | tf_op jit(solution)/shard_map/all_to_all | solution.py:79
  424.4 12.8 %all_to_all.50 = bf16[8,6,4096]{2,1,0:T(8,128)(2,1)S(1)} all-to-all(bf16[8,6,4096]{2,1,0:T(8,128)(2,1)S(1)} %all_to_all.41), channel_id=1, replica_groups=mesh['expert_0'=4,'expert_1'=2,'fsdp_0'=4,'fsdp_1'=4] {'expert_0','exper..., dimensions={0} | all-to-all | bytes 786432 | tf_op jit(solution)/shard_map/all_to_all | solution.py:81
  438.1 6.6 %copy.44 = bf16[1,512,4096]{1,2,0:T(8,128)(2,1)} copy(bf16[1,512,4096]{2,1,0:T(8,128)(2,1)} %param.13) | data formatting | bytes 8388608 | tf_op args[6]
  444.6 8.4 %fusion = (f32[]{:T(128)}, f32[]{:T(128)}, f32[]{:T(128)}) fusion(bf16[1,512,4096]{1,2,0:T(8,128)(2,1)} %copy.44, f32[]{:T(128)S(6)} %div.13, f32[1,512,4096]{1,2,0:T(8,128)} %get-tuple-element.46, f32[]{:T(128)S(6)} %div.12, bf16[1,512,4096]{1,2,0:T(8,128)(2,1)} %copy.40), kind=kLoop, calls=%fused_computation.8 | loop fusion | flops 25165824 | bytes 16777236 | tf_op jit(solution)/shard_map/reduce_sum | solution.py:52
  457.3 39.1 %all-gather.5.cloned.1.call-done = bf16[768,4096]{1,0:T(8,128)(2,1)} async-done(((bf16[48,4096]{1,0:T(8,128)(2,1)}), bf16[768,4096]{1,0:T(8,128)(2,1)}) %all-gather.5.cloned.1.call-update) | async-done | bytes 6291472 | tf_op jit(solution)/shard_map/all_gather | solution.py:84
  496.3 10.1 %fusion.8 = f32[]{:T(128)} fusion(bf16[768,4096]{1,0:T(8,128)(2,1)} %all-gather.5.cloned.1.call-done, f32[]{:T(128)} %bitcast.77, bf16[1,768,512]{2,1,0:T(8,128)(2,1)S(1)} %copy-done, f32[]{:T(128)S(6)} %div.13, f32[1,512,4096]{1,2,0:T(8,128)} %get-tuple-element.46, f32[]{:T(128)S(6)} %div.12, bf16[1,512,4096]{1,2,0:T(8,128)(2,1)} %copy.40), kind=kOutput, calls=%fused_computation.17 | convolution fusion | flops 3240099840 | bytes 19660816 | tf_op jit(solution)/shard_map/dot_general | solution.py:82
  507.8 10.7 %all-reduce.32 = (f32[4]{0:T(128)S(1)}, f32[4]{0:T(128)S(1)}, f32[4]{0:T(128)S(1)}, f32[4]{0:T(128)S(1)}) all-reduce(f32[4]{0:T(128)S(1)} %dynamic-update-slice.8, f32[4]{0:T(128)S(1)} %dynamic-update-slice.16, f32[4]{0:T(128)S(1)} %dynamic-update-slice.20, ...), channel_id=1, replica_groups=mesh['expert_0'=4,'expert_1'=2,'fsdp_0'=4,'fsdp_1'=4] {'expert_0'}, use_global_device_ids=true, to_apply=%add.8 | all-reduce | flops 16 | bytes 128
  537.1 10.4 %all-reduce.30 = (f32[4]{0:T(128)S(1)}, f32[4]{0:T(128)S(1)}, f32[4]{0:T(128)S(1)}, f32[4]{0:T(128)S(1)}) all-reduce(f32[4]{0:T(128)S(1)} %dynamic-update-slice.10, f32[4]{0:T(128)S(1)} %dynamic-update-slice.18, f32[4]{0:T(128)S(1)} %dynamic-update-slice.22, ...), channel_id=1, replica_groups=mesh['expert_0'=4,'expert_1'=2,'fsdp_0'=4,'fsdp_1'=4] {'fsdp_0'}, use_global_device_ids=true, to_apply=%add.10 | all-reduce | flops 16 | bytes 128
  555.4 8.6 %all-reduce.28 = (f32[4]{0:T(128)S(1)}, f32[4]{0:T(128)S(1)}, f32[4]{0:T(128)S(1)}, f32[4]{0:T(128)S(1)}) all-reduce(f32[4]{0:T(128)S(1)} %dynamic-update-slice.11, f32[4]{0:T(128)S(1)} %dynamic-update-slice.19, f32[4]{0:T(128)S(1)} %dynamic-update-slice.23, ...), channel_id=1, replica_groups=mesh['expert_0'=4,'expert_1'=2,'fsdp_0'=4,'fsdp_1'=4] {'fsdp_1'}, use_global_device_ids=true, to_apply=%add.11 | all-reduce | flops 16 | bytes 128
  566.6 7.7 %fusion.4 = f32[1,512,4096]{1,2,0:T(8,128)} fusion(bf16[1,512,4096]{1,2,0:T(8,128)(2,1)} %copy.40, f32[]{:T(128)S(6)} %div.14, f32[]{:T(128)S(6)} %div.12, f32[]{:T(128)S(6)} %div.13, f32[1,512,4096]{1,2,0:T(8,128)} %get-tuple-element.46), kind=kLoop, calls=%fused_computation.12 | loop fusion | flops 16777216 | bytes 20971532 | tf_op jit(solution)/shard_map/add | solution.py:91
  576.8 8.9 %copy.45 = f32[1,512,4096]{2,1,0:T(8,128)} copy(f32[1,512,4096]{1,2,0:T(8,128)} %fusion.4) | data formatting | bytes 16777216
  (136 shorter events, 79.0 us)
Async XLA Ops:
  7.2 1.1 copy-start
  7.2 107.4 %reduce-scatter.5.cloned.1.call-start = ((), (), s32[]{:S(2)}) async-start(), calls=%async_computation.6 | async-start | bytes 13369344 | tf_op jit(solution)/shard_map/reduce_scatter | solution.py:73
  16.9 104.5 %copy-start.1 = (s32[16,2]{0,1:T(2,128)S(1)}, s32[16,2]{0,1:T(2,128)}, u32[]{:S(2)}) copy-start(s32[16,2]{0,1:T(2,128)} %param.8) | copy-start | bytes 388
  16.9 105.2 %copy-start.3 = (f32[16,2]{0,1:T(2,128)S(1)}, f32[16,2]{0,1:T(2,128)}, u32[]{:S(2)}) copy-start(f32[16,2]{0,1:T(2,128)} %param.9) | copy-start | bytes 388
  16.9 120.5 %copy-start.2 = (f32[16]{0:T(128)S(1)}, f32[16]{0:T(128)}, u32[]{:S(2)}) copy-start(f32[16]{0:T(128)} %param.10) | copy-start | bytes 196
  116.7 43.0 %copy-start.7 = (u32[128]{0:T(128)S(1)}, u32[128]{0:T(128)}, u32[]{:S(2)}) copy-start(u32[128]{0:T(128)} %constant.24) | copy-start | bytes 1540
  116.7 20.5 %all-to-all-start = ((f32[8,6,4096]{2,1,0:T(8,128)}), f32[8,6,4096]{2,1,0:T(8,128)S(1)}, u32[]{:S(2)}, u32[]{:S(2)}) async-start(f32[8,6,4096]{2,1,0:T(8,128)} %all_to_all.32), calls=%async_computation.1 | async-start | bytes 2097152 | tf_op jit(solution)/shard_map/all_to_all | solution.py:79
  121.3 89.5 %all-gather.3.cloned.1.call-start = ((), (), s32[]{:S(2)}) async-start(), calls=%async_computation.7 | async-start | bytes 6684672 | tf_op jit(solution)/shard_map/all_gather | solution.py:84
  152.5 248.9 %reduce-scatter.7.cloned.1.call-start = ((), (), s32[]{:S(2)}) async-start(), calls=%async_computation.9 | async-start | bytes 13369344 | tf_op jit(solution)/shard_map/reduce_scatter | solution.py:73
  210.8 16.5 %copy-start.6 = (u32[128]{0:T(128)S(1)}, u32[128]{0:T(128)}, u32[]{:S(2)}) copy-start(u32[128]{0:T(128)} %constant.29) | copy-start | bytes 1540
  210.8 33.8 %copy-start.5 = (u32[128]{0:T(128)S(1)}, u32[128]{0:T(128)}, u32[]{:S(2)}) copy-start(u32[128]{0:T(128)} %constant.34) | copy-start | bytes 1540
  210.8 43.2 %copy-start.4 = (u32[128]{0:T(128)S(1)}, u32[128]{0:T(128)}, u32[]{:S(2)}) copy-start(u32[128]{0:T(128)} %constant.39) | copy-start | bytes 1540
  311.3 185.0 %all-gather.5.cloned.1.call-start = ((), (), s32[]{:S(2)}) async-start(), calls=%async_computation.8 | async-start | bytes 6684672 | tf_op jit(solution)/shard_map/all_gather | solution.py:84
Sparse Core Ops, SparseCore 0:
  17.0 97.4 reduce-scatter.4
  152.6 58.1 all-gather.2
  311.4 89.9 reduce-scatter.6
  438.2 58.0 all-gather.4
